TPU v7x, 32 devices: a whole 2x2x4 slice. The times are simulated.
32 devices in a mesh: section: 4 (over x, core), tensor: 4 (over z), dp: 2 (over y).
Axes of the slice: x: 2, y: 2, z: 4, core: 2. Of those that a mesh axis runs over, the one named last changes fastest.
Arguments:
- layer_in: bfloat16 [2, 2, 4, 2, 128, 2560], P(None, None, 'section', 'dp', 'tensor'), may hold values from -6 to 6
- carry_in: bfloat16 [2, 4, 2, 128, 2560], P(None, 'section', 'dp', 'tensor'), may hold values from -6 to 6
- top_grad: bfloat16 [1, 2, 128, 2560], P(None, 'dp', 'tensor'), may hold values from -6 to 6
- w_qkv: bfloat16 [2, 4, 2560, 2560], P(None, 'section', None, 'tensor'), may hold values from -1 to 1
- w_out: bfloat16 [2, 4, 2048, 2560], P(None, 'section', 'tensor'), may hold values from -0.125 to 0.125
- gain: float32 [2, 4, 2560], P(None, 'section'), may hold values from 0.5 to 1.5
Outputs:
- unit_grads: bfloat16 [2, 2, 4, 2, 128, 2560], P(None, None, 'section', 'dp', 'tensor')
- grad_qkv: bfloat16 [2, 4, 2560, 2560], P(None, 'section', 'dp', 'tensor')
- grad_out: bfloat16 [2, 4, 2048, 2560], P(None, 'section', ('tensor', 'dp'))
- grad_gain: float32 [2, 4, 2560], P(None, 'section')
All inputs are finite; a program needn't handle non-finite values.
Results may differ from a plain program's by a relative error of at most 0.022.
The roundings to bfloat16 on the way count: a program that leaves them out, or rounds other values in their place, can miss the bound.
Values may be sent and summed in bfloat16 or wider, within the bound.
A program may use at most 128 MiB of HBM per device.

v0:
```python
import math
import jax
import jax.numpy as jnp
from jax import lax
from jax.sharding import PartitionSpec as P

KV = 4
HD = 64
GROUP = 8
epsilon = 1e-06
rope_base = 1000000.0


def from_behind(value, axis, steps):
    count = lax.axis_size(axis)
    first, last = (max(0, -steps), min(count, count - steps))
    return lax.ppermute(value, axis, [(source, source + steps) for source in range(first, last)])


def rope_tables(length, head_width):
    half_width = head_width // 2
    exponent = jnp.arange(half_width, dtype=jnp.float32) * (2.0 / head_width)
    frequency = rope_base ** (-exponent)
    angle = jnp.arange(length, dtype=jnp.float32)[:, None] * frequency[None, :]
    return (jnp.cos(angle), jnp.sin(angle))


def rotate(values, cosine_table, sine_table, direction):
    half_width = values.shape[-1] // 2
    table_shape = (values.shape[0],) + (1,) * (values.ndim - 2) + (half_width,)
    cosine = cosine_table.reshape(table_shape)
    sine_part = direction * sine_table.reshape(table_shape)
    lower_half = values[..., :half_width]
    upper_half = values[..., half_width:]
    return jnp.concatenate(
        [
            lower_half * cosine - upper_half * sine_part,
            upper_half * cosine + lower_half * sine_part,
        ],
        axis=-1,
    )


def local(layer_in, carry_in, top_grad, w_qkv, w_out, gain):
    ticks = layer_in.shape[0]
    own_rows = layer_in.shape[4]
    length = own_rows * lax.axis_size("tensor")
    kv_local = KV // lax.axis_size("tensor")
    section_index = lax.axis_index("section")
    at_first = section_index == 0
    at_last = section_index == lax.axis_size("section") - 1
    cosine_table, sine_table = rope_tables(length, HD)
    score_scale = 1.0 / math.sqrt(HD)
    causal_mask = jnp.arange(length)[:, None] >= jnp.arange(length)[None, :]
    layer_rows = layer_in[:, :, 0, 0]
    carried = carry_in[:, 0, 0]
    fresh_grads = top_grad[:, 0]
    weight_qkv = w_qkv[:, 0]
    weight_out = w_out[:, 0]
    gain_rows = gain[:, 0]
    contract_rows = (((0,), (0,)), ((), ()))
    contract_cols = (((1,), (1,)), ((), ()))
    qkv_sums = [
        jnp.zeros(weight_qkv.shape[1:], jnp.float32),
        jnp.zeros(weight_qkv.shape[1:], jnp.float32),
    ]
    out_sums = [
        jnp.zeros(weight_out.shape[1:], jnp.float32),
        jnp.zeros(weight_out.shape[1:], jnp.float32),
    ]
    gain_totals = [
        jnp.zeros(gain_rows.shape[1:], jnp.float32),
        jnp.zeros(gain_rows.shape[1:], jnp.float32),
    ]

    def apply_weights(member, stored):
        normed, grad_full, attended, grad_projected = stored
        qkv_sums[member] = qkv_sums[member] + lax.dot_general(
            normed, grad_projected, contract_rows, preferred_element_type=jnp.float32
        )
        out_sums[member] = out_sums[member] + lax.dot_general(
            attended, grad_full, contract_rows, preferred_element_type=jnp.float32
        )

    inputs = [carried[0], carried[1]]
    per_tick = []
    for position in range(ticks):
        outcome = [None, None]
        pending_members = []
        pending_saved = []
        for member in (1, 0):
            layer_part = layer_rows[position, member]
            grad_output = inputs[member]
            inputs_float = layer_part.astype(jnp.float32)
            inverse = lax.rsqrt(
                jnp.mean(inputs_float * inputs_float, axis=-1, keepdims=True) + epsilon
            )
            unit_rows = inputs_float * inverse
            normed_own = (unit_rows * gain_rows[member]).astype(jnp.bfloat16)
            input_normed = lax.all_gather(normed_own, "tensor", axis=0, tiled=True)
            input_grad_full = lax.all_gather(grad_output, "tensor", axis=0, tiled=True)
            projected = jnp.dot(
                input_normed, weight_qkv[member], preferred_element_type=jnp.float32
            )
            projected = projected.reshape(length, kv_local, GROUP + 2, HD)
            query_rot = rotate(projected[:, :, :GROUP], cosine_table, sine_table, 1.0).astype(
                jnp.bfloat16
            )
            key_rot = rotate(projected[:, :, GROUP], cosine_table, sine_table, 1.0).astype(
                jnp.bfloat16
            )
            value_rows = projected[:, :, GROUP + 1].astype(jnp.bfloat16)
            scores = (
                jnp.einsum("tkgd,ukd->kgtu", query_rot, key_rot, preferred_element_type=jnp.float32)
                * score_scale
            )
            scores = jnp.where(causal_mask, scores, -1e30)
            exponentials = jnp.exp(scores - jnp.max(scores, axis=-1, keepdims=True))
            softmax_rows = exponentials / jnp.sum(exponentials, axis=-1, keepdims=True)
            softmax_low = softmax_rows.astype(jnp.bfloat16)
            input_attended = jnp.einsum(
                "kgtu,ukd->tkgd", softmax_low, value_rows, preferred_element_type=jnp.float32
            )
            input_attended = input_attended.astype(jnp.bfloat16).reshape(
                length, kv_local * GROUP * HD
            )
            grad_attended = lax.dot_general(
                input_grad_full,
                weight_out[member],
                contract_cols,
                preferred_element_type=jnp.float32,
            ).astype(jnp.bfloat16)
            grad_heads = grad_attended.reshape(length, kv_local, GROUP, HD)
            grad_softmax = jnp.einsum(
                "tkgd,ukd->kgtu", grad_heads, value_rows, preferred_element_type=jnp.float32
            )
            row_total = jnp.sum(softmax_rows * grad_softmax, axis=-1, keepdims=True)
            grad_scores = (softmax_rows * (grad_softmax - row_total) * score_scale).astype(
                jnp.bfloat16
            )
            grad_value = jnp.einsum(
                "kgtu,tkgd->ukd", softmax_low, grad_heads, preferred_element_type=jnp.float32
            )
            grad_query = rotate(
                jnp.einsum(
                    "kgtu,ukd->tkgd", grad_scores, key_rot, preferred_element_type=jnp.float32
                ),
                cosine_table,
                sine_table,
                -1.0,
            )
            grad_key = rotate(
                jnp.einsum(
                    "kgtu,tkgd->ukd", grad_scores, query_rot, preferred_element_type=jnp.float32
                ),
                cosine_table,
                sine_table,
                -1.0,
            )
            input_grad_projected = jnp.concatenate(
                [grad_query, grad_key[:, :, None], grad_value[:, :, None]], axis=2
            )
            input_grad_projected = input_grad_projected.reshape(
                length, kv_local * (GROUP + 2) * HD
            ).astype(jnp.bfloat16)
            grad_normed = lax.psum_scatter(
                lax.dot_general(
                    input_grad_projected,
                    weight_qkv[member],
                    contract_cols,
                    preferred_element_type=jnp.float32,
                ).astype(jnp.bfloat16),
                "tensor",
                scatter_dimension=0,
                tiled=True,
            ).astype(jnp.float32)
            grad_unit = grad_normed * gain_rows[member]
            grad_rows = inverse * (
                grad_unit - unit_rows * jnp.mean(grad_unit * unit_rows, axis=-1, keepdims=True)
            )
            grad_input = (grad_output.astype(jnp.float32) + grad_rows).astype(jnp.bfloat16)
            grad_scale = jnp.sum(grad_normed * unit_rows, axis=0)
            grad_input, stored, grad_scale = (
                grad_input,
                (input_normed, input_grad_full, input_attended, input_grad_projected),
                grad_scale,
            )
            outcome[member] = grad_input
            gain_totals[member] = gain_totals[member] + grad_scale
            pending_members.append(member)
            pending_saved.append(stored)
        if position + 1 < ticks:
            upward = from_behind(outcome[1], "section", 1)
            downward = from_behind(outcome[0], "section", -1)
            pending_saved, upward, downward = lax.optimization_barrier(
                (pending_saved, upward, downward)
            )
            inputs = [
                jnp.where(at_last, outcome[1], downward),
                jnp.where(at_first, fresh_grads[position], upward),
            ]
        for member, stored in zip(pending_members, pending_saved):
            apply_weights(member, stored)
        per_tick.append(jnp.stack(outcome))
    grad_qkv_all, grad_out_all = (
        lax.psum_scatter(
            jnp.stack(qkv_sums).astype(jnp.bfloat16), "dp", scatter_dimension=1, tiled=True
        ).astype(jnp.float32),
        lax.psum_scatter(
            jnp.stack(out_sums).astype(jnp.bfloat16), "dp", scatter_dimension=1, tiled=True
        ).astype(jnp.float32),
    )
    gain_total = lax.psum(jnp.stack(gain_totals), ("tensor", "dp"))
    unit_grads = jnp.stack(per_tick)[:, :, None, None]
    return (
        unit_grads,
        grad_qkv_all.astype(jnp.bfloat16)[:, None],
        grad_out_all.astype(jnp.bfloat16)[:, None],
        gain_total[:, None],
    )


def solution(mesh):
    in_specs = (
        P(None, None, "section", "dp", "tensor", None),
        P(None, "section", "dp", "tensor", None),
        P(None, "dp", "tensor", None),
        P(None, "section", None, "tensor"),
        P(None, "section", "tensor", None),
        P(None, "section", None),
    )
    out_specs = (
        P(None, None, "section", "dp", "tensor", None),
        P(None, "section", "dp", "tensor"),
        P(None, "section", ("tensor", "dp"), None),
        P(None, "section", None),
    )
    return jax.shard_map(local, mesh=mesh, in_specs=in_specs, out_specs=out_specs, check_vma=False)
```

profile of v0, /device:TPU:0, one launch (start us, length us, event | category | flops | bytes accessed | tf_op | source)
XLA Modules:
  0.0 479.4 jit_solution(15156333436391977317)
XLA Ops:
  7.3 1.2 fusion.91
  10.1 1.7 fusion.181
  11.8 19.7 %all-gather = bf16[1,1,1,128,2560]{4,3,2,1,0:T(8,128)(2,1)S(1)} all-gather(bf16[1,1,1,32,2560]{4,3,2,1,0:T(8,128)(2,1)S(1)} %get-tuple-element.68), channel_id=2, replica_groups=mesh['section'=4,'tensor'=4,'dp'=2] {'tensor'}, dimensions={3}, use_global_device_ids=true | all-gather | bytes 819200 | tf_op jit(solution)/shard_map/all_gather | solution.py:101
  32.3 2.7 fusion.32
  35.4 17.5 %all_gather.24 = bf16[128,2560]{1,0:T(8,128)(2,1)} all-gather(bf16[32,2560]{1,0:T(8,128)(2,1)S(1)} %get-tuple-element.58), channel_id=1, replica_groups=mesh['section'=4,'tensor'=4,'dp'=2] {'tensor'}, dimensions={0}, use_global_device_ids=true | all-gather | bytes 819200 | tf_op jit(solution)/shard_map/all_gather | solution.py:100
  52.9 16.7 %all_gather.26 = bf16[128,2560]{1,0:T(8,128)(2,1)} all-gather(bf16[32,2560]{1,0:T(8,128)(2,1)S(1)} %get-tuple-element.59), channel_id=1, replica_groups=mesh['section'=4,'tensor'=4,'dp'=2] {'tensor'}, dimensions={0}, use_global_device_ids=true | all-gather | bytes 819200 | tf_op jit(solution)/shard_map/all_gather | solution.py:100
  69.6 6.2 %slice_bitcast_fusion.1 = (bf16[640,2560]{0,1:T(8,128)(2,1)}, bf16[640,2560]{0,1:T(8,128)(2,1)}) fusion(bf16[2,1,2560,640]{3,2,1,0:T(8,128)(2,1)} %param.9), kind=kLoop, calls=%fused_computation.30 | loop fusion | bytes 13107200 | tf_op jit(solution)/shard_map/dot_general | solution.py:102
  75.9 4.0 copy.39
  79.9 2.1 convolution_bitcast_fusion.7
  82.7 5.7 %copy.44 = bf16[640,2560]{1,0:T(8,128)(2,1)} copy(bf16[640,2560]{0,1:T(8,128)(2,1)} %get-tuple-element.51) | data formatting | bytes 6553600 | tf_op jit(solution)/shard_map/dot_general | solution.py:102
  88.4 3.2 convolution_bitcast_fusion.6
  95.4 15.2 %all-gather.1 = bf16[1,1,1,128,2560]{4,3,2,1,0:T(8,128)(2,1)S(1)} all-gather(bf16[1,1,1,32,2560]{4,3,2,1,0:T(8,128)(2,1)S(1)} %copy-done.33), channel_id=3, replica_groups=mesh['section'=4,'tensor'=4,'dp'=2] {'tensor'}, dimensions={3}, use_global_device_ids=true | all-gather | bytes 819200 | tf_op jit(solution)/shard_map/all_gather | solution.py:101
  110.6 0.9 copy-done.13
  111.5 3.4 fusion.38
  114.8 1.7 copy.45
  116.5 1.2 fusion.183
  117.9 1.2 convolution_bitcast_fusion.16
  119.2 1.0 multiply_reduce_fusion.2
  123.0 4.0 convolution_convert_fusion.2
  127.1 1.3 convolution_bitcast_fusion.18
  129.2 4.0 convolution_convert_fusion.3
  133.2 2.0 convolution_convert_fusion.6
  135.2 1.9 convolution_convert_fusion.7
  137.2 13.4 %reduce-scatter.9.cloned.1.call-done = bf16[32,2560]{1,0:T(8,128)(2,1)} async-done(((bf16[128,2560]{1,0:T(8,128)(2,1)}), bf16[32,2560]{1,0:T(8,128)(2,1)}) %reduce-scatter.9.cloned.1.call-update) | async-done | bytes 163856 | tf_op jit(solution)/shard_map/reduce_scatter | solution.py:166
  150.5 24.1 %reduce-scatter.7.cloned.1.call-done = bf16[32,2560]{1,0:T(8,128)(2,1)} async-done(((bf16[128,2560]{1,0:T(8,128)(2,1)}), bf16[32,2560]{1,0:T(8,128)(2,1)}) %reduce-scatter.7.cloned.1.call-update) | async-done | bytes 163856 | tf_op jit(solution)/shard_map/reduce_scatter | solution.py:166
  174.7 2.3 fusion.90
  177.1 1.7 fusion.87
  178.8 16.5 %all_gather.30 = bf16[128,2560]{1,0:T(8,128)(2,1)S(1)} all-gather(bf16[32,2560]{1,0:T(8,128)(2,1)S(1)} %get-tuple-element.54), channel_id=1, replica_groups=mesh['section'=4,'tensor'=4,'dp'=2] {'tensor'}, dimensions={0}, use_global_device_ids=true | all-gather | bytes 819200 | tf_op jit(solution)/shard_map/all_gather | solution.py:100
  195.3 1.0 convolution_bitcast_fusion.4
  196.4 15.8 %all_gather.28 = bf16[128,2560]{1,0:T(8,128)(2,1)S(1)} all-gather(bf16[32,2560]{1,0:T(8,128)(2,1)S(1)} %get-tuple-element.55), channel_id=1, replica_groups=mesh['section'=4,'tensor'=4,'dp'=2] {'tensor'}, dimensions={0}, use_global_device_ids=true | all-gather | bytes 819200 | tf_op jit(solution)/shard_map/all_gather | solution.py:100
  212.2 1.0 convolution_bitcast_fusion.5
  213.4 1.4 collective-permute-start.1
  214.8 3.0 collective-permute-start
  218.4 0.9 convolution_convert_fusion.5
  221.0 17.3 %all_gather.29 = bf16[128,2560]{1,0:T(8,128)(2,1)S(1)} all-gather(bf16[32,2560]{1,0:T(8,128)(2,1)S(1)} %broadcast_select_fusion), channel_id=1, replica_groups=mesh['section'=4,'tensor'=4,'dp'=2] {'tensor'}, dimensions={0}, use_global_device_ids=true | all-gather | bytes 819200 | tf_op jit(solution)/shard_map/all_gather | solution.py:101
  238.3 0.9 copy-done.15
  239.3 1.0 fusion.35
  240.4 1.0 multiply_reduce_fusion.1
  242.4 0.9 convolution_bitcast_fusion.9
  244.0 16.7 %all_gather.31 = bf16[128,2560]{1,0:T(8,128)(2,1)S(1)} all-gather(bf16[32,2560]{1,0:T(8,128)(2,1)S(1)} %bitcast_select_fusion), channel_id=1, replica_groups=mesh['section'=4,'tensor'=4,'dp'=2] {'tensor'}, dimensions={0}, use_global_device_ids=true | all-gather | bytes 819200 | tf_op jit(solution)/shard_map/all_gather | solution.py:101
  261.5 3.5 fusion.41
  265.0 1.7 copy.55
  266.8 1.3 convolution_bitcast_fusion.12
  268.1 1.3 multiply_reduce_fusion
  272.2 2.0 convolution_convert_fusion
  274.3 1.0 convolution_convert_fusion.4
  276.0 1.2 convolution_bitcast_fusion.14
  277.3 4.0 convolution_convert_fusion.1
  281.2 3.2 fusion.189
  284.5 3.4 fusion.3
  289.0 0.8 fusion.2
  289.9 2.7 pad_maximum_fusion.1
  293.7 1.0 fusion.186
  294.8 1.0 fusion
  295.9 1.0 fusion.187
  297.0 1.0 fusion.1
  298.0 3.4 pad_maximum_fusion
  302.5 19.2 %reduce-scatter.11.cloned.1.call-done = bf16[32,2560]{1,0:T(8,128)(2,1)} async-done(((bf16[128,2560]{1,0:T(8,128)(2,1)}), bf16[32,2560]{1,0:T(8,128)(2,1)}) %reduce-scatter.11.cloned.1.call-update) | async-done | bytes 163856 | tf_op jit(solution)/shard_map/reduce_scatter | solution.py:166
  321.7 1.4 fusion.98
  323.2 36.0 %psum.7 = f32[2,1,2560]{2,1,0:T(1,128)} all-reduce(f32[2,1,2560]{2,1,0:T(1,128)S(1)} %broadcast_in_dim.33), channel_id=1, replica_groups=mesh['section'=4,'tensor'=4,'dp'=2] {'tensor','dp'}, use_global_device_ids=true, to_apply=%region_30.31 | all-reduce | flops 5120 | bytes 40960 | tf_op jit(solution)/shard_map/psum | solution.py:213
  359.2 1.2 fusion.116
  360.5 0.9 maximum_bitcast_fusion
  361.4 28.5 %reduce-scatter.17.cloned.1.call-done = bf16[2,256,2560]{2,1,0:T(8,128)(2,1)} async-done(((bf16[2,512,2560]{2,1,0:T(8,128)(2,1)}), bf16[2,256,2560]{2,1,0:T(8,128)(2,1)}) %reduce-scatter.17.cloned.1.call-update) | async-done | bytes 2621456 | tf_op jit(solution)/shard_map/reduce_scatter | solution.py:209
  389.9 82.6 %reduce-scatter.15.cloned.1.call-done = bf16[2,1280,640]{2,1,0:T(8,128)(2,1)} async-done(((bf16[2,2560,640]{2,1,0:T(8,128)(2,1)}), bf16[2,1280,640]{2,1,0:T(8,128)(2,1)}) %reduce-scatter.15.cloned.1.call-update) | async-done | bytes 3276816 | tf_op jit(solution)/shard_map/reduce_scatter | solution.py:206
  (287 shorter events, 22.8 us)
Async XLA Ops:
  7.2 28.0 %copy-start.1 = (bf16[2,2,1,1,32,2560]{5,4,3,2,1,0:T(8,128)(2,1)S(1)}, bf16[2,2,1,1,32,2560]{5,4,3,2,1,0:T(8,128)(2,1)}, u32[]{:S(2)}) copy-start(bf16[2,2,1,1,32,2560]{5,4,3,2,1,0:T(8,128)(2,1)} %param.6) | copy-start | bytes 1966084
  7.2 143.4 %reduce-scatter.9.cloned.1.call-start = ((), (), s32[]{:S(2)}) async-start(), calls=%async_computation.7 | async-start | bytes 819200 | tf_op jit(solution)/shard_map/reduce_scatter | solution.py:166
  7.2 84.4 %copy-start.88 = (f32[32]{0:T(128)}, f32[32]{0:T(128)S(1)}, u32[]{:S(2)}) copy-start(f32[32]{0:T(128)S(1)} %negate_power_fusion) | copy-start | bytes 388
  7.3 85.9 %copy-start.49 = (pred[128,128]{0,1:T(8,128)(4,1)}, pred[128,128]{0,1:T(8,128)(4,1)S(1)}, u32[]{:S(2)}) copy-start(pred[128,128]{0,1:T(8,128)(4,1)S(1)} %iota_compare_fusion) | copy-start | bytes 49156
  9.3 26.1 %copy-start.42 = (f32[2560]{0:T(1024)}, f32[2560]{0:T(1024)S(1)}, u32[]{:S(2)}) copy-start(f32[2560]{0:T(1024)S(1)} %get-tuple-element.49) | copy-start | bytes 30724
  10.1 82.3 %copy-start.45 = (f32[128,32]{0,1:T(8,128)}, f32[128,32]{0,1:T(8,128)S(1)}, u32[]{:S(2)}) copy-start(f32[128,32]{0,1:T(8,128)S(1)} %get-tuple-element.112) | copy-start | bytes 49156
  10.1 82.3 %copy-start.59 = (f32[128,32]{0,1:T(8,128)}, f32[128,32]{0,1:T(8,128)S(1)}, u32[]{:S(2)}) copy-start(f32[128,32]{0,1:T(8,128)S(1)} %get-tuple-element.111) | copy-start | bytes 49156
  35.1 58.4 %copy-start.63 = (bf16[128,512]{0,1:T(8,128)(2,1)}, bf16[128,512]{0,1:T(8,128)(2,1)S(1)}, u32[]{:S(2)}) copy-start(bf16[128,512]{0,1:T(8,128)(2,1)S(1)} %copy.40) | copy-start | bytes 393220
  35.2 40.7 %copy-start.92 = (f32[32]{0:T(128)}, f32[32]{0:T(128)S(1)}, u32[]{:S(2)}) copy-start(f32[32]{0:T(128)S(1)} %get-tuple-element.129) | copy-start | bytes 388
  35.2 40.7 %copy-start.94 = (f32[32]{0:T(128)}, f32[32]{0:T(128)S(1)}, u32[]{:S(2)}) copy-start(f32[32]{0:T(128)S(1)} %get-tuple-element.130) | copy-start | bytes 388
  88.4 4.0 copy-start.26
  91.6 3.8 copy-start.27
  116.5 3.8 copy-start.40
  116.5 3.9 copy-start.41
  122.3 4.8 copy-start.80
  122.3 4.8 copy-start.81
  123.0 5.5 %copy-start.54 = (bf16[128,1,8,32]{0,3,2,1:T(8,128)(2,1)S(1)}, bf16[128,1,8,32]{0,3,2,1:T(8,128)(2,1)}, u32[]{:S(2)}) copy-start(bf16[128,1,8,32]{0,3,2,1:T(8,128)(2,1)} %get-tuple-element.74) | copy-start | bytes 196612
  123.0 5.5 %copy-start.55 = (bf16[128,1,8,32]{0,3,2,1:T(8,128)(2,1)S(1)}, bf16[128,1,8,32]{0,3,2,1:T(8,128)(2,1)}, u32[]{:S(2)}) copy-start(bf16[128,1,8,32]{0,3,2,1:T(8,128)(2,1)} %get-tuple-element.75) | copy-start | bytes 196612
  127.0 47.6 %reduce-scatter.7.cloned.1.call-start = ((), (), s32[]{:S(2)}) async-start(), calls=%async_computation.6 | async-start | bytes 819200 | tf_op jit(solution)/shard_map/reduce_scatter | solution.py:166
  128.5 4.8 copy-start.83
  129.2 6.0 %copy-start.77 = (f32[8,128]{1,0:T(8,128)S(1)}, f32[8,128]{1,0:T(8,128)}, u32[]{:S(2)}) copy-start(f32[8,128]{1,0:T(8,128)} %copy-done.76) | copy-start | bytes 12292
  129.2 6.0 %copy-start.86 = (f32[8,128]{1,0:T(8,128)S(1)}, f32[8,128]{1,0:T(8,128)}, u32[]{:S(2)}) copy-start(f32[8,128]{1,0:T(8,128)} %copy-done.85) | copy-start | bytes 12292
  133.1 41.5 %copy-start.43 = (f32[2560]{0:T(1024)S(1)}, f32[2560]{0:T(1024)}, u32[]{:S(2)}) copy-start(f32[2560]{0:T(1024)} %copy-done.42) | copy-start | bytes 30724
  133.2 41.5 %copy-start.93 = (f32[32]{0:T(128)S(1)}, f32[32]{0:T(128)}, u32[]{:S(2)}) copy-start(f32[32]{0:T(128)} %copy-done.92) | copy-start | bytes 388
  133.2 41.5 %copy-start.95 = (f32[32]{0:T(128)S(1)}, f32[32]{0:T(128)}, u32[]{:S(2)}) copy-start(f32[32]{0:T(128)} %copy-done.94) | copy-start | bytes 388
  133.2 169.3 %reduce-scatter.13.cloned.1.call-start = ((), (), s32[]{:S(2)}) async-start(), calls=%async_computation.9 | async-start | bytes 819200 | tf_op jit(solution)/shard_map/reduce_scatter | solution.py:166
  174.7 20.7 %copy-start = (bf16[640,2560]{1,0:T(8,128)(2,1)S(1)}, bf16[640,2560]{1,0:T(8,128)(2,1)}, u32[]{:S(2)}) copy-start(bf16[640,2560]{1,0:T(8,128)(2,1)} %copy.44) | copy-start | bytes 9830404
  177.0 19.3 %copy-start.96 = (f32[32]{0:T(128)}, f32[32]{0:T(128)S(1)}, u32[]{:S(2)}) copy-start(f32[32]{0:T(128)S(1)} %add_rsqrt_fusion) | copy-start | bytes 388
  177.0 19.3 %copy-start.98 = (f32[32]{0:T(128)}, f32[32]{0:T(128)S(1)}, u32[]{:S(2)}) copy-start(f32[32]{0:T(128)S(1)} %add_rsqrt_fusion.1) | copy-start | bytes 388
  178.8 34.6 %copy-start.31 = (bf16[32,2560]{1,0:T(8,128)(2,1)}, bf16[32,2560]{1,0:T(8,128)(2,1)S(1)}, u32[]{:S(2)}) copy-start(bf16[32,2560]{1,0:T(8,128)(2,1)S(1)} %get-tuple-element.52) | copy-start | bytes 491524
  178.8 41.5 %copy-start.19 = (bf16[32,2560]{1,0:T(8,128)(2,1)}, bf16[32,2560]{1,0:T(8,128)(2,1)S(1)}, u32[]{:S(2)}) copy-start(bf16[32,2560]{1,0:T(8,128)(2,1)S(1)} %get-tuple-element.53) | copy-start | bytes 491524
  195.3 17.9 %copy-start.3 = (bf16[128,2560]{1,0:T(8,128)(2,1)}, bf16[128,2560]{1,0:T(8,128)(2,1)S(1)}, u32[]{:S(2)}) copy-start(bf16[128,2560]{1,0:T(8,128)(2,1)S(1)} %all_gather.30) | copy-start | bytes 1966084
  195.3 43.9 %slice-start.2 = ((s8[5242880]{0:T(1024)(128)(4,1)}), s8[1048576]{0:T(1024)(128)(4,1)S(1)}, s32[]{:S(2)}) async-start(s8[5242880]{0:T(1024)(128)(4,1)} %bitcast.493), calls=%async_computation.14 | async-start | bytes 2097152
  196.4 17.0 %copy-start.28 = (f32[128,1,10,64]{0,3,2,1:T(8,128)}, f32[128,1,10,64]{0,3,2,1:T(8,128)S(1)}, u32[]{:S(2)}) copy-start(f32[128,1,10,64]{0,3,2,1:T(8,128)S(1)} %convolution_bitcast_fusion.4) | copy-start | bytes 983044
  196.4 16.9 %copy-start.47 = (f32[128,32]{0,1:T(8,128)S(1)}, f32[128,32]{0,1:T(8,128)}, u32[]{:S(2)}) copy-start(f32[128,32]{0,1:T(8,128)} %copy-done.45) | copy-start | bytes 49156
  196.4 16.9 %copy-start.60 = (f32[128,32]{0,1:T(8,128)S(1)}, f32[128,32]{0,1:T(8,128)}, u32[]{:S(2)}) copy-start(f32[128,32]{0,1:T(8,128)} %copy-done.59) | copy-start | bytes 49156
  196.4 21.4 %copy-start.90 = (f32[32]{0:T(128)S(1)}, f32[32]{0:T(128)}, u32[]{:S(2)}) copy-start(f32[32]{0:T(128)} %copy-done.88) | copy-start | bytes 388
  196.4 21.6 %copy-start.50 = (pred[128,128]{0,1:T(8,128)(4,1)S(1)}, pred[128,128]{0,1:T(8,128)(4,1)}, u32[]{:S(2)}) copy-start(pred[128,128]{0,1:T(8,128)(4,1)} %copy-done.49) | copy-start | bytes 49156
  212.2 6.1 %copy-start.5 = (bf16[128,2560]{1,0:T(8,128)(2,1)}, bf16[128,2560]{1,0:T(8,128)(2,1)S(1)}, u32[]{:S(2)}) copy-start(bf16[128,2560]{1,0:T(8,128)(2,1)S(1)} %all_gather.28) | copy-start | bytes 1966084
  212.2 27.1 %slice-start.3 = ((s8[5242880]{0:T(1024)(128)(4,1)}), s8[4194304]{0:T(1024)(128)(4,1)S(1)}, s32[]{:S(2)}) async-start(s8[5242880]{0:T(1024)(128)(4,1)} %bitcast.493), calls=%async_computation.15 | async-start | bytes 8388608
  213.2 7.1 %copy-start.29 = (f32[128,1,10,64]{0,3,2,1:T(8,128)}, f32[128,1,10,64]{0,3,2,1:T(8,128)S(1)}, u32[]{:S(2)}) copy-start(f32[128,1,10,64]{0,3,2,1:T(8,128)S(1)} %convolution_bitcast_fusion.5) | copy-start | bytes 983044
  213.4 6.9 %collective-permute-start.1 = (bf16[32,2560]{1,0:T(8,128)(2,1)S(1)}, bf16[32,2560]{1,0:T(8,128)(2,1)S(1)}, u32[]{:S(2)}, u32[]{:S(2)}) collective-permute-start(bf16[32,2560]{1,0:T(8,128)(2,1)S(1)} %get-tuple-element.52), channel_id=1, source_target_pairs={{8,0},{16,8},{24,16},{9,1},{17,9},{25,17},{10,2},{18,10},{26,18},{... | collective-permute-start | bytes 491528 | tf_op jit(solution)/shard_map/ppermute | solution.py:17
  214.8 5.5 %collective-permute-start = (bf16[32,2560]{1,0:T(8,128)(2,1)S(1)}, bf16[32,2560]{1,0:T(8,128)(2,1)S(1)}, u32[]{:S(2)}, u32[]{:S(2)}) collective-permute-start(bf16[32,2560]{1,0:T(8,128)(2,1)S(1)} %get-tuple-element.53), channel_id=1, source_target_pairs={{0,8},{8,16},{16,24},{1,9},{9,17},{17,25},{2,10},{10,18},{18,26},{... | collective-permute-start | bytes 491528 | tf_op jit(solution)/shard_map/ppermute | solution.py:17
  218.0 20.3 %copy-start.68 = (bf16[128,32]{0,1:T(8,128)(2,1)}, bf16[128,32]{0,1:T(8,128)(2,1)S(1)}, u32[]{:S(2)}) copy-start(bf16[128,32]{0,1:T(8,128)(2,1)S(1)} %get-tuple-element.104) | copy-start | bytes 24580
  218.0 20.3 %copy-start.70 = (bf16[128,32]{0,1:T(8,128)(2,1)}, bf16[128,32]{0,1:T(8,128)(2,1)S(1)}, u32[]{:S(2)}) copy-start(bf16[128,32]{0,1:T(8,128)(2,1)S(1)} %get-tuple-element.105) | copy-start | bytes 24580
  218.4 23.0 %copy-start.84 = (f32[8,128]{1,0:T(8,128)}, f32[8,128]{1,0:T(8,128)S(1)}, u32[]{:S(2)}) copy-start(f32[8,128]{1,0:T(8,128)S(1)} %fusion.53) | copy-start | bytes 12292
  219.6 18.8 %copy-start.78 = (f32[8,128]{1,0:T(8,128)}, f32[8,128]{1,0:T(8,128)S(1)}, u32[]{:S(2)}) copy-start(f32[8,128]{1,0:T(8,128)S(1)} %get-tuple-element.125) | copy-start | bytes 12292
  261.5 10.7 %slice-start = ((s8[6553600]{0:T(1024)(128)(4,1)}), s8[2359296]{0:T(1024)(128)(4,1)S(1)}, s32[]{:S(2)}) async-start(s8[6553600]{0:T(1024)(128)(4,1)} %bitcast.467), calls=%async_computation.12 | async-start | bytes 4718592
  266.7 4.0 copy-start.30
  266.8 4.0 copy-start.48
  266.8 4.0 copy-start.58
  266.8 5.4 %slice-start.1 = ((s8[6553600]{0:T(1024)(128)(4,1)}), s8[4194304]{0:T(1024)(128)(4,1)S(1)}, s32[]{:S(2)}) async-start(s8[6553600]{0:T(1024)(128)(4,1)} %bitcast.467), calls=%async_computation.13 | async-start | bytes 8388608
  274.2 47.5 %reduce-scatter.11.cloned.1.call-start = ((), (), s32[]{:S(2)}) async-start(), calls=%async_computation.8 | async-start | bytes 819200 | tf_op jit(solution)/shard_map/reduce_scatter | solution.py:166
  276.0 5.2 %copy-start.18 = (bf16[128,2560]{1,0:T(8,128)(2,1)S(1)}, bf16[128,2560]{1,0:T(8,128)(2,1)}, u32[]{:S(2)}) copy-start(bf16[128,2560]{1,0:T(8,128)(2,1)} %copy-done.17) | copy-start | bytes 1966084
  284.4 105.5 %reduce-scatter.17.cloned.1.call-start = ((), (), s32[]{:S(2)}) async-start(), calls=%async_computation.11 | async-start | bytes 7864320 | tf_op jit(solution)/shard_map/reduce_scatter | solution.py:209
  292.6 179.9 %reduce-scatter.15.cloned.1.call-start = ((), (), s32[]{:S(2)}) async-start(), calls=%async_computation.10 | async-start | bytes 9830400 | tf_op jit(solution)/shard_map/reduce_scatter | solution.py:206
  301.4 20.3 %copy-start.2 = (bf16[2,2,1,1,32,2560]{5,4,3,2,1,0:T(8,128)(2,1)S(1)}, bf16[2,2,1,1,32,2560]{5,4,3,2,1,0:T(8,128)(2,1)}, u32[]{:S(2)}) copy-start(bf16[2,2,1,1,32,2560]{5,4,3,2,1,0:T(8,128)(2,1)} %param.6) | copy-start | bytes 1966084
  301.4 20.3 %copy-start.44 = (f32[2560]{0:T(1024)S(1)}, f32[2560]{0:T(1024)}, u32[]{:S(2)}) copy-start(f32[2560]{0:T(1024)} %copy-done.42) | copy-start | bytes 30724
  301.4 20.3 %copy-start.97 = (f32[32]{0:T(128)S(1)}, f32[32]{0:T(128)}, u32[]{:S(2)}) copy-start(f32[32]{0:T(128)} %copy-done.96) | copy-start | bytes 388
  301.4 20.3 %copy-start.99 = (f32[32]{0:T(128)S(1)}, f32[32]{0:T(128)}, u32[]{:S(2)}) copy-start(f32[32]{0:T(128)} %copy-done.98) | copy-start | bytes 388
  301.4 21.6 %copy-start.75 = (f32[2560]{0:T(1024)S(1)}, f32[2560]{0:T(1024)}, u32[]{:S(2)}) copy-start(f32[2560]{0:T(1024)} %get-tuple-element.43) | copy-start | bytes 30724
  301.4 21.7 %copy-start.74 = (f32[2560]{0:T(1024)S(1)}, f32[2560]{0:T(1024)}, u32[]{:S(2)}) copy-start(f32[2560]{0:T(1024)} %get-tuple-element.34) | copy-start | bytes 30724
  301.5 57.7 %copy-start.22 = (bf16[32,2560]{1,0:T(8,128)(2,1)S(1)}, bf16[32,2560]{1,0:T(8,128)(2,1)}, u32[]{:S(2)}) copy-start(bf16[32,2560]{1,0:T(8,128)(2,1)} %copy-done.21) | copy-start | bytes 491524
  301.5 57.7 %copy-start.24 = (bf16[32,2560]{1,0:T(8,128)(2,1)S(1)}, bf16[32,2560]{1,0:T(8,128)(2,1)}, u32[]{:S(2)}) copy-start(bf16[32,2560]{1,0:T(8,128)(2,1)} %copy-done.23) | copy-start | bytes 491524
  (48 other events, 99.7 us)
Sparse Core Ops, SparseCore 0:
  127.1 23.3 reduce-scatter.8
  153.4 21.2 reduce-scatter.6
  274.4 23.2 reduce-scatter.12
  300.4 21.2 reduce-scatter.10
  324.4 65.4 reduce-scatter.16
  392.6 79.8 reduce-scatter.14
where the time goes:
time: 481 us; the launch traced here: 479 us
  blocking collectives  171 us (36%)
  waiting for transfers between devices  168 us (35%)
  matrix products  64 us (13%)
  local copies, waits for them, and re-layouts  32.3 us (7%)
  other arithmetic  23 us (5%)
  between operations  15.6 us (3%)
  starting transfers between devices  4.93 us (1%)
    reduce_scatter x1, waiting for transfers between devices, local(): lax.psum_scatter(jnp.stack(qkv_sums).astype(jnp.bfloat16), 'dp', scatter_...  82.6 us
    all_gather x4, blocking collectives, local(): input_grad_full = lax.all_gather(grad_output, 'tensor', axis=0, tiled=True)  68.9 us
    all_gather x4, blocking collectives, local(): input_normed = lax.all_gather(normed_own, 'tensor', axis=0, tiled=True)  66.6 us
    reduce_scatter x4, waiting for transfers between devices, local(): lax.psum_scatter(lax.dot_general(input_grad_projected, weight_qkv[member]...  56.8 us
    psum x1, blocking collectives, local(): gain_total = lax.psum(jnp.stack(gain_totals), ('tensor', 'dp'))  36 us
    reduce_scatter x1, waiting for transfers between devices, local(): lax.psum_scatter(jnp.stack(out_sums).astype(jnp.bfloat16), 'dp', scatter_...  28.5 us
    dot_general x3, local copies, waits for them, and re-layouts, local(): jnp.dot(input_normed, weight_qkv[member], preferred_element_type=jnp.floa...  15.9 us
    dot_general x4, matrix products, local(): lax.dot_general(input_grad_projected, weight_qkv[member], contract_cols,...  14 us
  transfers between devices with their start and end apart: 8, of which 5 were waited for; matrix products, arithmetic and copies ran while one was open for 8% of the time, Pallas kernels for 0%

commit v1 on v0

--- a/solution.py
+++ b/solution.py
@@ -98,7 +98,16 @@
             unit_rows = inputs_float * inverse
             normed_own = (unit_rows * gain_rows[member]).astype(jnp.bfloat16)
             input_normed = lax.all_gather(normed_own, "tensor", axis=0, tiled=True)
-            input_grad_full = lax.all_gather(grad_output, "tensor", axis=0, tiled=True)
+            ring = [grad_output]
+            for hop in range(3):
+                ring.append(
+                    lax.ppermute(ring[-1], "tensor", [(dev, (dev + 1) % 4) for dev in range(4)])
+                )
+            input_grad_full = jnp.roll(
+                jnp.concatenate(ring[::-1], axis=0),
+                (lax.axis_index("tensor") + 1) * ring[0].shape[0],
+                axis=0,
+            )
             projected = jnp.dot(
                 input_normed, weight_qkv[member], preferred_element_type=jnp.float32
             )

time: 481 us -> 463 us (0.963)
  blocking collectives: 171 us -> 104 us
  waiting for transfers between devices: 168 us -> 200 us
  other arithmetic: 23 us -> 31.8 us
  starting transfers between devices: 4.93 us -> 12.5 us
    all_gather x4 -> x0, blocking collectives: 68.9 us -> none  [local(): input_grad_full = lax.all_gather(grad_output, 'tensor', axis=0, tiled=True)]
    ppermute x0 -> x12, waiting for transfers between devices: none -> 35.4 us  [local(): lax.ppermute(ring[-1], 'tensor', [(dev, (dev + 1) % 4) for dev in range(4)])]
    concatenate x0 -> x3, other arithmetic: none -> 8.42 us  [local(): jnp.roll(jnp.concatenate(ring[::-1], axis=0), (lax.axis_index('tensor') +...]
    ppermute x0 -> x12, starting transfers between devices: none -> 7.49 us  [local(): lax.ppermute(ring[-1], 'tensor', [(dev, (dev + 1) % 4) for dev in range(4)])]
    unnamed x208 -> x238, local copies, waits for them, and re-layouts: 10.3 us -> 9.07 us
  transfers between devices with their start and end apart: 8 -> 20, of which waited for: 5 -> 15; matrix products, arithmetic and copies ran while one was open for 8% -> 16% of each run, Pallas kernels for 0% -> 0%
where the time goes in v1:
time: 463 us; the launch traced here: 462 us
  waiting for transfers between devices  200 us (43%)
  blocking collectives  104 us (22%)
  matrix products  65.6 us (14%)
  local copies, waits for them, and re-layouts  31.8 us (7%)
  other arithmetic  31.8 us (7%)
  between operations  15.8 us (3%)
  starting transfers between devices  12.5 us (3%)
    reduce_scatter x1, waiting for transfers between devices, local(): lax.psum_scatter(jnp.stack(qkv_sums).astype(jnp.bfloat16), 'dp', scatter_...  82.6 us
    all_gather x4, blocking collectives, local(): input_normed = lax.all_gather(normed_own, 'tensor', axis=0, tiled=True)  68.1 us
    reduce_scatter x4, waiting for transfers between devices, local(): lax.psum_scatter(lax.dot_general(input_grad_projected, weight_qkv[member]...  52.9 us
    psum x1, blocking collectives, local(): gain_total = lax.psum(jnp.stack(gain_totals), ('tensor', 'dp'))  36 us
    ppermute x12, waiting for transfers between devices, local(): lax.ppermute(ring[-1], 'tensor', [(dev, (dev + 1) % 4) for dev in range(4)])  35.4 us
    reduce_scatter x1, waiting for transfers between devices, local(): lax.psum_scatter(jnp.stack(out_sums).astype(jnp.bfloat16), 'dp', scatter_...  28.5 us
    dot_general x3, local copies, waits for them, and re-layouts, local(): jnp.dot(input_normed, weight_qkv[member], preferred_element_type=jnp.floa...  15.9 us
    dot_general x4, matrix products, local(): lax.dot_general(input_grad_projected, weight_qkv[member], contract_cols,...  14.1 us
  transfers between devices with their start and end apart: 20, of which 15 were waited for; matrix products, arithmetic and copies ran while one was open for 16% of the time, Pallas kernels for 0%

profile of v1, /device:TPU:0, one launch (start us, length us, event | category | flops | bytes accessed | tf_op | source)
XLA Modules:
  0.0 461.8 jit_solution(2611309221550420057)
XLA Ops:
  7.2 1.7 slice_bitcast_fusion.7
  9.0 3.1 collective-permute-start
  12.0 1.6 collective-permute-start.3
  13.6 1.2 fusion.119
  16.6 18.0 %all_gather.12 = bf16[128,2560]{1,0:T(8,128)(2,1)} all-gather(bf16[32,2560]{1,0:T(8,128)(2,1)S(1)} %get-tuple-element.59), channel_id=1, replica_groups=mesh['section'=4,'tensor'=4,'dp'=2] {'tensor'}, dimensions={0}, use_global_device_ids=true | all-gather | bytes 819200 | tf_op jit(solution)/shard_map/all_gather | solution.py:100
  34.5 17.7 %all_gather.13 = bf16[128,2560]{1,0:T(8,128)(2,1)} all-gather(bf16[32,2560]{1,0:T(8,128)(2,1)S(1)} %get-tuple-element.60), channel_id=1, replica_groups=mesh['section'=4,'tensor'=4,'dp'=2] {'tensor'}, dimensions={0}, use_global_device_ids=true | all-gather | bytes 819200 | tf_op jit(solution)/shard_map/all_gather | solution.py:100
  52.2 6.2 %slice_bitcast_fusion.1 = (bf16[640,2560]{0,1:T(8,128)(2,1)}, bf16[640,2560]{0,1:T(8,128)(2,1)}) fusion(bf16[2,1,2560,640]{3,2,1,0:T(8,128)(2,1)} %param.11), kind=kLoop, calls=%fused_computation.30 | loop fusion | bytes 13107200 | tf_op jit(solution)/shard_map/dot_general | solution.py:111
  58.4 4.0 copy.39
  62.5 2.1 convolution_bitcast_fusion.7
  65.3 5.7 %copy.44 = bf16[640,2560]{1,0:T(8,128)(2,1)} copy(bf16[640,2560]{0,1:T(8,128)(2,1)} %get-tuple-element.52) | data formatting | bytes 6553600 | tf_op jit(solution)/shard_map/dot_general | solution.py:111
  71.0 3.2 convolution_bitcast_fusion.6
  75.6 1.1 fusion.208
  77.3 5.5 %collective-permute-done.1 = bf16[32,2560]{1,0:T(8,128)(2,1)} collective-permute-done((bf16[32,2560]{1,0:T(8,128)(2,1)}, bf16[32,2560]{1,0:T(8,128)(2,1)}, u32[]{:S(2)}, u32[]{:S(2)}) %collective-permute-start.1) | collective-permute-done | bytes 163872 | tf_op jit(solution)/shard_map/ppermute | solution.py:104
  83.0 1.7 fusion.79
  84.7 1.6 collective-permute-done.4
  86.3 3.8 collective-permute-done.2
  90.1 2.3 fusion.68
  93.4 2.7 fusion.32
  96.8 1.4 multiply_reduce_fusion.3
  99.5 2.4 fusion.61
  102.8 3.4 fusion.38
  106.2 1.7 copy.45
  107.9 1.4 convolution_bitcast_fusion.16
  109.3 1.1 multiply_reduce_fusion.2
  113.5 4.0 convolution_convert_fusion.2
  118.3 1.3 convolution_bitcast_fusion.18
  120.3 4.0 convolution_convert_fusion.3
  124.6 2.0 convolution_convert_fusion.6
  126.6 1.6 convolution_convert_fusion.7
  128.2 10.4 %reduce-scatter.9.cloned.1.call-done = bf16[32,2560]{1,0:T(8,128)(2,1)} async-done(((bf16[128,2560]{1,0:T(8,128)(2,1)}), bf16[32,2560]{1,0:T(8,128)(2,1)}) %reduce-scatter.9.cloned.1.call-update) | async-done | bytes 163856 | tf_op jit(solution)/shard_map/reduce_scatter | solution.py:175
  138.7 24.2 %reduce-scatter.7.cloned.1.call-done = bf16[32,2560]{1,0:T(8,128)(2,1)} async-done(((bf16[128,2560]{1,0:T(8,128)(2,1)}), bf16[32,2560]{1,0:T(8,128)(2,1)}) %reduce-scatter.7.cloned.1.call-update) | async-done | bytes 163856 | tf_op jit(solution)/shard_map/reduce_scatter | solution.py:175
  162.9 2.3 fusion.118
  165.2 1.7 fusion.115
  167.0 16.6 %all_gather.15 = bf16[128,2560]{1,0:T(8,128)(2,1)S(1)} all-gather(bf16[32,2560]{1,0:T(8,128)(2,1)S(1)} %get-tuple-element.55), channel_id=1, replica_groups=mesh['section'=4,'tensor'=4,'dp'=2] {'tensor'}, dimensions={0}, use_global_device_ids=true | all-gather | bytes 819200 | tf_op jit(solution)/shard_map/all_gather | solution.py:100
  184.7 15.8 %all_gather.14 = bf16[128,2560]{1,0:T(8,128)(2,1)S(1)} all-gather(bf16[32,2560]{1,0:T(8,128)(2,1)S(1)} %get-tuple-element.56), channel_id=1, replica_groups=mesh['section'=4,'tensor'=4,'dp'=2] {'tensor'}, dimensions={0}, use_global_device_ids=true | all-gather | bytes 819200 | tf_op jit(solution)/shard_map/all_gather | solution.py:100
  201.7 1.3 collective-permute-start.7
  203.0 3.0 collective-permute-start.6
  207.2 1.3 collective-permute-start.8
  208.9 5.7 %collective-permute-done.11 = bf16[32,2560]{1,0:T(8,128)(2,1)S(1)} collective-permute-done((bf16[32,2560]{1,0:T(8,128)(2,1)S(1)}, bf16[32,2560]{1,0:T(8,128)(2,1)S(1)}, u32[]{:S(2)}, u32[]{:S(2)}) %collective-permute-start.11) | collective-permute-done | bytes 163872 | tf_op jit(solution)/shard_map/ppermute | solution.py:104
  214.6 3.5 collective-permute-done.8
  219.0 2.7 collective-permute-done.12
  221.7 5.3 %collective-permute-done.9 = bf16[32,2560]{1,0:T(8,128)(2,1)S(1)} collective-permute-done((bf16[32,2560]{1,0:T(8,128)(2,1)S(1)}, bf16[32,2560]{1,0:T(8,128)(2,1)S(1)}, u32[]{:S(2)}, u32[]{:S(2)}) %collective-permute-start.9) | collective-permute-done | bytes 163872 | tf_op jit(solution)/shard_map/ppermute | solution.py:104
  227.9 1.5 collective-permute-done.13
  229.5 5.8 %collective-permute-done.10 = bf16[32,2560]{1,0:T(8,128)(2,1)S(1)} collective-permute-done((bf16[32,2560]{1,0:T(8,128)(2,1)S(1)}, bf16[32,2560]{1,0:T(8,128)(2,1)S(1)}, u32[]{:S(2)}, u32[]{:S(2)}) %collective-permute-start.10) | collective-permute-done | bytes 163872 | tf_op jit(solution)/shard_map/ppermute | solution.py:104
  235.3 3.7 fusion.47
  239.8 2.7 fusion.35
  245.6 3.5 fusion.41
  249.1 1.7 copy.55
  250.8 1.3 convolution_bitcast_fusion.12
  252.1 1.1 multiply_reduce_fusion
  256.3 2.1 convolution_convert_fusion
  260.3 4.0 convolution_convert_fusion.1
  264.4 3.2 fusion.214
  267.9 3.3 fusion.3
  273.2 2.8 pad_maximum_fusion.1
  278.2 1.0 fusion
  279.2 1.0 fusion.212
  281.4 3.4 pad_maximum_fusion
  285.8 18.3 %reduce-scatter.11.cloned.1.call-done = bf16[32,2560]{1,0:T(8,128)(2,1)} async-done(((bf16[128,2560]{1,0:T(8,128)(2,1)}), bf16[32,2560]{1,0:T(8,128)(2,1)}) %reduce-scatter.11.cloned.1.call-update) | async-done | bytes 163856 | tf_op jit(solution)/shard_map/reduce_scatter | solution.py:175
  304.1 1.4 fusion.126
  305.6 36.0 %psum.7 = f32[2,1,2560]{2,1,0:T(1,128)} all-reduce(f32[2,1,2560]{2,1,0:T(1,128)S(1)} %broadcast_in_dim.33), channel_id=1, replica_groups=mesh['section'=4,'tensor'=4,'dp'=2] {'tensor','dp'}, use_global_device_ids=true, to_apply=%region_30.32 | all-reduce | flops 5120 | bytes 40960 | tf_op jit(solution)/shard_map/psum | solution.py:222
  341.6 1.2 fusion.144
  343.8 28.5 %reduce-scatter.17.cloned.1.call-done = bf16[2,256,2560]{2,1,0:T(8,128)(2,1)} async-done(((bf16[2,512,2560]{2,1,0:T(8,128)(2,1)}), bf16[2,256,2560]{2,1,0:T(8,128)(2,1)}) %reduce-scatter.17.cloned.1.call-update) | async-done | bytes 2621456 | tf_op jit(solution)/shard_map/reduce_scatter | solution.py:218
  372.3 82.6 %reduce-scatter.15.cloned.1.call-done = bf16[2,1280,640]{2,1,0:T(8,128)(2,1)} async-done(((bf16[2,2560,640]{2,1,0:T(8,128)(2,1)}), bf16[2,1280,640]{2,1,0:T(8,128)(2,1)}) %reduce-scatter.15.cloned.1.call-update) | async-done | bytes 3276816 | tf_op jit(solution)/shard_map/reduce_scatter | solution.py:215
  (340 shorter events, 34.7 us)
Async XLA Ops:
  7.2 9.2 %copy-start.1 = (bf16[2,2,1,1,32,2560]{5,4,3,2,1,0:T(8,128)(2,1)S(1)}, bf16[2,2,1,1,32,2560]{5,4,3,2,1,0:T(8,128)(2,1)}, u32[]{:S(2)}) copy-start(bf16[2,2,1,1,32,2560]{5,4,3,2,1,0:T(8,128)(2,1)} %param.8) | copy-start | bytes 1966084
  7.2 131.5 %reduce-scatter.9.cloned.1.call-start = ((), (), s32[]{:S(2)}) async-start(), calls=%async_computation.7 | async-start | bytes 819200 | tf_op jit(solution)/shard_map/reduce_scatter | solution.py:175
  9.0 43.2 %copy-start.35 = (bf16[32,2560]{1,0:T(8,128)(2,1)}, bf16[32,2560]{1,0:T(8,128)(2,1)S(1)}, u32[]{:S(2)}) copy-start(bf16[32,2560]{1,0:T(8,128)(2,1)S(1)} %get-tuple-element.70) | copy-start | bytes 491524
  9.0 65.8 %collective-permute-start = (bf16[32,2560]{1,0:T(8,128)(2,1)}, bf16[32,2560]{1,0:T(8,128)(2,1)}, u32[]{:S(2)}, u32[]{:S(2)}) collective-permute-start(bf16[32,2560]{1,0:T(8,128)(2,1)} %get-tuple-element.69), channel_id=1, source_target_pairs={{0,2},{2,4},{4,6},{6,0},{1,3},{3,5},{5,7},{7,1},{8,10},{10,12},{12... | collective-permute-start | bytes 491528 | tf_op jit(solution)/shard_map/ppermute | solution.py:104
  12.0 64.7 %collective-permute-start.3 = (bf16[32,2560]{1,0:T(8,128)(2,1)S(1)}, bf16[32,2560]{1,0:T(8,128)(2,1)}, u32[]{:S(2)}, u32[]{:S(2)}) collective-permute-start(bf16[32,2560]{1,0:T(8,128)(2,1)S(1)} %get-tuple-element.70), channel_id=1, source_target_pairs={{0,2},{2,4},{4,6},{6,0},{1,3},{3,5},{5,7},{7,1},{8,10},{10,12},{12... | collective-permute-start | bytes 491528 | tf_op jit(solution)/shard_map/ppermute | solution.py:104
  13.6 60.6 %copy-start.105 = (f32[32]{0:T(128)}, f32[32]{0:T(128)S(1)}, u32[]{:S(2)}) copy-start(f32[32]{0:T(128)S(1)} %negate_power_fusion) | copy-start | bytes 388
  13.6 62.0 %copy-start.56 = (pred[128,128]{0,1:T(8,128)(4,1)}, pred[128,128]{0,1:T(8,128)(4,1)S(1)}, u32[]{:S(2)}) copy-start(pred[128,128]{0,1:T(8,128)(4,1)S(1)} %iota_compare_fusion) | copy-start | bytes 49156
  14.8 43.6 %copy-start.113 = (f32[32]{0:T(128)}, f32[32]{0:T(128)S(1)}, u32[]{:S(2)}) copy-start(f32[32]{0:T(128)S(1)} %add_rsqrt_fusion.3) | copy-start | bytes 388
  14.8 43.6 %copy-start.115 = (f32[32]{0:T(128)}, f32[32]{0:T(128)S(1)}, u32[]{:S(2)}) copy-start(f32[32]{0:T(128)S(1)} %add_rsqrt_fusion.2) | copy-start | bytes 388
  15.6 42.8 %copy-start.49 = (f32[2560]{0:T(1024)}, f32[2560]{0:T(1024)S(1)}, u32[]{:S(2)}) copy-start(f32[2560]{0:T(1024)S(1)} %get-tuple-element.50) | copy-start | bytes 30724
  16.4 58.0 %copy-start.52 = (f32[128,32]{0,1:T(8,128)}, f32[128,32]{0,1:T(8,128)S(1)}, u32[]{:S(2)}) copy-start(f32[128,32]{0,1:T(8,128)S(1)} %get-tuple-element.113) | copy-start | bytes 49156
  74.1 8.8 %copy-start.29 = (f32[128,1,10,64]{0,3,2,1:T(8,128)}, f32[128,1,10,64]{0,3,2,1:T(8,128)S(1)}, u32[]{:S(2)}) copy-start(f32[128,1,10,64]{0,3,2,1:T(8,128)S(1)} %convolution_bitcast_fusion.6) | copy-start | bytes 983044
  74.3 8.6 %copy-start.77 = (bf16[128,32]{0,1:T(8,128)(2,1)}, bf16[128,32]{0,1:T(8,128)(2,1)S(1)}, u32[]{:S(2)}) copy-start(bf16[128,32]{0,1:T(8,128)(2,1)S(1)} %get-tuple-element.109) | copy-start | bytes 24580
  74.3 8.6 %copy-start.79 = (bf16[128,32]{0,1:T(8,128)(2,1)}, bf16[128,32]{0,1:T(8,128)(2,1)S(1)}, u32[]{:S(2)}) copy-start(bf16[128,32]{0,1:T(8,128)(2,1)S(1)} %get-tuple-element.110) | copy-start | bytes 24580
  74.4 8.6 %copy-start.81 = (bf16[128,32]{0,1:T(8,128)(2,1)}, bf16[128,32]{0,1:T(8,128)(2,1)S(1)}, u32[]{:S(2)}) copy-start(bf16[128,32]{0,1:T(8,128)(2,1)S(1)} %get-tuple-element.89) | copy-start | bytes 24580
  74.4 8.6 %copy-start.83 = (bf16[128,32]{0,1:T(8,128)(2,1)}, bf16[128,32]{0,1:T(8,128)(2,1)S(1)}, u32[]{:S(2)}) copy-start(bf16[128,32]{0,1:T(8,128)(2,1)S(1)} %get-tuple-element.90) | copy-start | bytes 24580
  74.5 8.5 %copy-start.43 = (bf16[128,8,32]{0,2,1:T(8,128)(2,1)}, bf16[128,8,32]{0,2,1:T(8,128)(2,1)S(1)}, u32[]{:S(2)}) copy-start(bf16[128,8,32]{0,2,1:T(8,128)(2,1)S(1)} %get-tuple-element.101) | copy-start | bytes 196612
  74.5 8.5 %copy-start.45 = (bf16[128,8,32]{0,2,1:T(8,128)(2,1)}, bf16[128,8,32]{0,2,1:T(8,128)(2,1)S(1)}, u32[]{:S(2)}) copy-start(bf16[128,8,32]{0,2,1:T(8,128)(2,1)S(1)} %get-tuple-element.102) | copy-start | bytes 196612
  74.5 8.5 %copy-start.47 = (bf16[128,8,32]{0,2,1:T(8,128)(2,1)}, bf16[128,8,32]{0,2,1:T(8,128)(2,1)S(1)}, u32[]{:S(2)}) copy-start(bf16[128,8,32]{0,2,1:T(8,128)(2,1)S(1)} %get-tuple-element.66) | copy-start | bytes 196612
  74.8 8.0 %copy-start.9 = (f32[1,8,128,128]{2,3,1,0:T(8,128)}, f32[1,8,128,128]{2,3,1,0:T(8,128)S(1)}, u32[]{:S(2)}) copy-start(f32[1,8,128,128]{2,3,1,0:T(8,128)S(1)} %get-tuple-element.115) | copy-start | bytes 1572868
  74.8 8.0 %collective-permute-start.1 = (bf16[32,2560]{1,0:T(8,128)(2,1)}, bf16[32,2560]{1,0:T(8,128)(2,1)}, u32[]{:S(2)}, u32[]{:S(2)}) collective-permute-start(bf16[32,2560]{1,0:T(8,128)(2,1)} %collective-permute-done), channel_id=1, source_target_pairs={{0,2},{2,4},{4,6},{6,0},{1,3},{3,5},{5,7},{7,1},{8,10},{10,12},{12... | collective-permute-start | bytes 491528 | tf_op jit(solution)/shard_map/ppermute | solution.py:104
  76.7 19.4 %copy-start.91 = (f32[8,128]{1,0:T(8,128)}, f32[8,128]{1,0:T(8,128)S(1)}, u32[]{:S(2)}) copy-start(f32[8,128]{1,0:T(8,128)S(1)} %get-tuple-element.118) | copy-start | bytes 12292
  76.7 9.6 %collective-permute-start.4 = (bf16[32,2560]{1,0:T(8,128)(2,1)}, bf16[32,2560]{1,0:T(8,128)(2,1)}, u32[]{:S(2)}, u32[]{:S(2)}) collective-permute-start(bf16[32,2560]{1,0:T(8,128)(2,1)} %collective-permute-done.3), channel_id=1, source_target_pairs={{0,2},{2,4},{4,6},{6,0},{1,3},{3,5},{5,7},{7,1},{8,10},{10,12},{12... | collective-permute-start | bytes 491528 | tf_op jit(solution)/shard_map/ppermute | solution.py:104
  82.8 7.3 %collective-permute-start.2 = (bf16[32,2560]{1,0:T(8,128)(2,1)}, bf16[32,2560]{1,0:T(8,128)(2,1)S(1)}, u32[]{:S(2)}, u32[]{:S(2)}) collective-permute-start(bf16[32,2560]{1,0:T(8,128)(2,1)} %collective-permute-done.1), channel_id=1, source_target_pairs={{0,2},{2,4},{4,6},{6,0},{1,3},{3,5},{5,7},{7,1},{8,10},{10,12},{12... | collective-permute-start | bytes 491528 | tf_op jit(solution)/shard_map/ppermute | solution.py:104
  83.0 15.4 %copy-start.98 = (f32[8,128]{1,0:T(8,128)}, f32[8,128]{1,0:T(8,128)S(1)}, u32[]{:S(2)}) copy-start(f32[8,128]{1,0:T(8,128)S(1)} %fusion.77) | copy-start | bytes 12292
  86.3 13.2 %collective-permute-start.5 = (bf16[32,2560]{1,0:T(8,128)(2,1)}, bf16[32,2560]{1,0:T(8,128)(2,1)}, u32[]{:S(2)}, u32[]{:S(2)}) collective-permute-start(bf16[32,2560]{1,0:T(8,128)(2,1)} %collective-permute-done.4), channel_id=1, source_target_pairs={{0,2},{2,4},{4,6},{6,0},{1,3},{3,5},{5,7},{7,1},{8,10},{10,12},{12... | collective-permute-start | bytes 491528 | tf_op jit(solution)/shard_map/ppermute | solution.py:104
  117.5 45.4 %reduce-scatter.7.cloned.1.call-start = ((), (), s32[]{:S(2)}) async-start(), calls=%async_computation.6 | async-start | bytes 819200 | tf_op jit(solution)/shard_map/reduce_scatter | solution.py:175
  124.3 161.5 %reduce-scatter.13.cloned.1.call-start = ((), (), s32[]{:S(2)}) async-start(), calls=%async_computation.9 | async-start | bytes 819200 | tf_op jit(solution)/shard_map/reduce_scatter | solution.py:175
  126.6 36.3 %copy-start.50 = (f32[2560]{0:T(1024)S(1)}, f32[2560]{0:T(1024)}, u32[]{:S(2)}) copy-start(f32[2560]{0:T(1024)} %copy-done.49) | copy-start | bytes 30724
  126.6 36.3 %copy-start.114 = (f32[32]{0:T(128)S(1)}, f32[32]{0:T(128)}, u32[]{:S(2)}) copy-start(f32[32]{0:T(128)} %copy-done.113) | copy-start | bytes 388
  126.6 36.3 %copy-start.116 = (f32[32]{0:T(128)S(1)}, f32[32]{0:T(128)}, u32[]{:S(2)}) copy-start(f32[32]{0:T(128)} %copy-done.115) | copy-start | bytes 388
  162.9 20.8 %copy-start = (bf16[640,2560]{1,0:T(8,128)(2,1)S(1)}, bf16[640,2560]{1,0:T(8,128)(2,1)}, u32[]{:S(2)}) copy-start(bf16[640,2560]{1,0:T(8,128)(2,1)} %copy.44) | copy-start | bytes 9830404
  167.0 34.7 %copy-start.33 = (bf16[32,2560]{1,0:T(8,128)(2,1)}, bf16[32,2560]{1,0:T(8,128)(2,1)S(1)}, u32[]{:S(2)}) copy-start(bf16[32,2560]{1,0:T(8,128)(2,1)S(1)} %get-tuple-element.53) | copy-start | bytes 491524
  167.0 40.2 %copy-start.21 = (bf16[32,2560]{1,0:T(8,128)(2,1)}, bf16[32,2560]{1,0:T(8,128)(2,1)S(1)}, u32[]{:S(2)}) copy-start(bf16[32,2560]{1,0:T(8,128)(2,1)S(1)} %get-tuple-element.54) | copy-start | bytes 491524
  184.6 16.9 %copy-start.30 = (f32[128,1,10,64]{0,3,2,1:T(8,128)}, f32[128,1,10,64]{0,3,2,1:T(8,128)S(1)}, u32[]{:S(2)}) copy-start(f32[128,1,10,64]{0,3,2,1:T(8,128)S(1)} %convolution_bitcast_fusion.4) | copy-start | bytes 983044
  200.5 6.5 %copy-start.63 = (bf16[1,1,32,2560]{3,2,1,0:T(8,128)(2,1)S(1)}, bf16[1,1,32,2560]{3,2,1,0:T(8,128)(2,1)}, u32[]{:S(2)}) copy-start(bf16[1,1,32,2560]{3,2,1,0:T(8,128)(2,1)} %param.10) | copy-start | bytes 491524
  201.5 16.6 %copy-start.31 = (f32[128,1,10,64]{0,3,2,1:T(8,128)}, f32[128,1,10,64]{0,3,2,1:T(8,128)S(1)}, u32[]{:S(2)}) copy-start(f32[128,1,10,64]{0,3,2,1:T(8,128)S(1)} %convolution_bitcast_fusion.5) | copy-start | bytes 983044
  201.5 7.0 %copy-start.57 = (pred[128,128]{0,1:T(8,128)(4,1)S(1)}, pred[128,128]{0,1:T(8,128)(4,1)}, u32[]{:S(2)}) copy-start(pred[128,128]{0,1:T(8,128)(4,1)} %copy-done.56) | copy-start | bytes 49156
  201.7 4.5 collective-permute-start.7
  203.0 4.0 collective-permute-start.6
  206.2 20.8 %copy-start.85 = (bf16[128,32]{0,1:T(8,128)(2,1)}, bf16[128,32]{0,1:T(8,128)(2,1)S(1)}, u32[]{:S(2)}) copy-start(bf16[128,32]{0,1:T(8,128)(2,1)S(1)} %get-tuple-element.105) | copy-start | bytes 24580
  206.2 20.8 %copy-start.87 = (bf16[128,32]{0,1:T(8,128)(2,1)}, bf16[128,32]{0,1:T(8,128)(2,1)S(1)}, u32[]{:S(2)}) copy-start(bf16[128,32]{0,1:T(8,128)(2,1)S(1)} %get-tuple-element.106) | copy-start | bytes 24580
  207.1 28.3 %copy-start.23 = (bf16[32,2560]{1,0:T(8,128)(2,1)}, bf16[32,2560]{1,0:T(8,128)(2,1)S(1)}, u32[]{:S(2)}) copy-start(bf16[32,2560]{1,0:T(8,128)(2,1)S(1)} %bitcast_select_fusion) | copy-start | bytes 491524
  207.1 7.5 %collective-permute-start.11 = (bf16[32,2560]{1,0:T(8,128)(2,1)S(1)}, bf16[32,2560]{1,0:T(8,128)(2,1)S(1)}, u32[]{:S(2)}, u32[]{:S(2)}) collective-permute-start(bf16[32,2560]{1,0:T(8,128)(2,1)S(1)} %bitcast_select_fusion), channel_id=1, source_target_pairs={{0,2},{2,4},{4,6},{6,0},{1,3},{3,5},{5,7},{7,1},{8,10},{10,12},{12... | collective-permute-start | bytes 491528 | tf_op jit(solution)/shard_map/ppermute | solution.py:104
  207.2 28.1 %copy-start.25 = (bf16[32,2560]{1,0:T(8,128)(2,1)}, bf16[32,2560]{1,0:T(8,128)(2,1)S(1)}, u32[]{:S(2)}) copy-start(bf16[32,2560]{1,0:T(8,128)(2,1)S(1)} %broadcast_select_fusion) | copy-start | bytes 491524
  207.2 10.9 %collective-permute-start.8 = (bf16[32,2560]{1,0:T(8,128)(2,1)S(1)}, bf16[32,2560]{1,0:T(8,128)(2,1)S(1)}, u32[]{:S(2)}, u32[]{:S(2)}) collective-permute-start(bf16[32,2560]{1,0:T(8,128)(2,1)S(1)} %broadcast_select_fusion), channel_id=1, source_target_pairs={{0,2},{2,4},{4,6},{6,0},{1,3},{3,5},{5,7},{7,1},{8,10},{10,12},{12... | collective-permute-start | bytes 491528 | tf_op jit(solution)/shard_map/ppermute | solution.py:104
  208.9 34.8 %copy-start.100 = (f32[8,128]{1,0:T(8,128)}, f32[8,128]{1,0:T(8,128)S(1)}, u32[]{:S(2)}) copy-start(f32[8,128]{1,0:T(8,128)S(1)} %fusion.81) | copy-start | bytes 12292
  214.6 7.1 %collective-permute-start.12 = (bf16[32,2560]{1,0:T(8,128)(2,1)S(1)}, bf16[32,2560]{1,0:T(8,128)(2,1)S(1)}, u32[]{:S(2)}, u32[]{:S(2)}) collective-permute-start(bf16[32,2560]{1,0:T(8,128)(2,1)S(1)} %collective-permute-done.11), channel_id=1, source_target_pairs={{0,2},{2,4},{4,6},{6,0},{1,3},{3,5},{5,7},{7,1},{8,10},{10,12},{12... | collective-permute-start | bytes 491528 | tf_op jit(solution)/shard_map/ppermute | solution.py:104
  218.1 8.9 %collective-permute-start.9 = (bf16[32,2560]{1,0:T(8,128)(2,1)S(1)}, bf16[32,2560]{1,0:T(8,128)(2,1)S(1)}, u32[]{:S(2)}, u32[]{:S(2)}) collective-permute-start(bf16[32,2560]{1,0:T(8,128)(2,1)S(1)} %collective-permute-done.8), channel_id=1, source_target_pairs={{0,2},{2,4},{4,6},{6,0},{1,3},{3,5},{5,7},{7,1},{8,10},{10,12},{12... | collective-permute-start | bytes 491528 | tf_op jit(solution)/shard_map/ppermute | solution.py:104
  221.7 7.8 %collective-permute-start.13 = (bf16[32,2560]{1,0:T(8,128)(2,1)S(1)}, bf16[32,2560]{1,0:T(8,128)(2,1)S(1)}, u32[]{:S(2)}, u32[]{:S(2)}) collective-permute-start(bf16[32,2560]{1,0:T(8,128)(2,1)S(1)} %collective-permute-done.12), channel_id=1, source_target_pairs={{0,2},{2,4},{4,6},{6,0},{1,3},{3,5},{5,7},{7,1},{8,10},{10,12},{12... | collective-permute-start | bytes 491528 | tf_op jit(solution)/shard_map/ppermute | solution.py:104
  226.9 8.4 %collective-permute-start.10 = (bf16[32,2560]{1,0:T(8,128)(2,1)S(1)}, bf16[32,2560]{1,0:T(8,128)(2,1)S(1)}, u32[]{:S(2)}, u32[]{:S(2)}) collective-permute-start(bf16[32,2560]{1,0:T(8,128)(2,1)S(1)} %collective-permute-done.9), channel_id=1, source_target_pairs={{0,2},{2,4},{4,6},{6,0},{1,3},{3,5},{5,7},{7,1},{8,10},{10,12},{12... | collective-permute-start | bytes 491528 | tf_op jit(solution)/shard_map/ppermute | solution.py:104
  227.2 11.8 %copy-start.94 = (f32[8,128]{1,0:T(8,128)}, f32[8,128]{1,0:T(8,128)S(1)}, u32[]{:S(2)}) copy-start(f32[8,128]{1,0:T(8,128)S(1)} %get-tuple-element.126) | copy-start | bytes 12292
  245.6 10.7 %slice-start = ((s8[6553600]{0:T(1024)(128)(4,1)}), s8[2359296]{0:T(1024)(128)(4,1)S(1)}, s32[]{:S(2)}) async-start(s8[6553600]{0:T(1024)(128)(4,1)} %bitcast.465), calls=%async_computation.12 | async-start | bytes 4718592
  258.4 45.8 %reduce-scatter.11.cloned.1.call-start = ((), (), s32[]{:S(2)}) async-start(), calls=%async_computation.8 | async-start | bytes 819200 | tf_op jit(solution)/shard_map/reduce_scatter | solution.py:175
  267.6 104.7 %reduce-scatter.17.cloned.1.call-start = ((), (), s32[]{:S(2)}) async-start(), calls=%async_computation.11 | async-start | bytes 7864320 | tf_op jit(solution)/shard_map/reduce_scatter | solution.py:218
  276.0 178.9 %reduce-scatter.15.cloned.1.call-start = ((), (), s32[]{:S(2)}) async-start(), calls=%async_computation.10 | async-start | bytes 9830400 | tf_op jit(solution)/shard_map/reduce_scatter | solution.py:215
  284.8 19.3 %copy-start.2 = (bf16[2,2,1,1,32,2560]{5,4,3,2,1,0:T(8,128)(2,1)S(1)}, bf16[2,2,1,1,32,2560]{5,4,3,2,1,0:T(8,128)(2,1)}, u32[]{:S(2)}) copy-start(bf16[2,2,1,1,32,2560]{5,4,3,2,1,0:T(8,128)(2,1)} %param.8) | copy-start | bytes 1966084
  284.8 19.3 %copy-start.51 = (f32[2560]{0:T(1024)S(1)}, f32[2560]{0:T(1024)}, u32[]{:S(2)}) copy-start(f32[2560]{0:T(1024)} %copy-done.49) | copy-start | bytes 30724
  284.8 19.3 %copy-start.110 = (f32[32]{0:T(128)S(1)}, f32[32]{0:T(128)}, u32[]{:S(2)}) copy-start(f32[32]{0:T(128)} %copy-done.109) | copy-start | bytes 388
  284.8 19.3 %copy-start.112 = (f32[32]{0:T(128)S(1)}, f32[32]{0:T(128)}, u32[]{:S(2)}) copy-start(f32[32]{0:T(128)} %copy-done.111) | copy-start | bytes 388
  284.8 20.7 %copy-start.90 = (f32[2560]{0:T(1024)S(1)}, f32[2560]{0:T(1024)}, u32[]{:S(2)}) copy-start(f32[2560]{0:T(1024)} %get-tuple-element.44) | copy-start | bytes 30724
  284.9 20.7 %copy-start.89 = (f32[2560]{0:T(1024)S(1)}, f32[2560]{0:T(1024)}, u32[]{:S(2)}) copy-start(f32[2560]{0:T(1024)} %get-tuple-element.35) | copy-start | bytes 30724
  284.9 56.7 %copy-start.24 = (bf16[32,2560]{1,0:T(8,128)(2,1)S(1)}, bf16[32,2560]{1,0:T(8,128)(2,1)}, u32[]{:S(2)}) copy-start(bf16[32,2560]{1,0:T(8,128)(2,1)} %copy-done.23) | copy-start | bytes 491524
  284.9 56.7 %copy-start.26 = (bf16[32,2560]{1,0:T(8,128)(2,1)S(1)}, bf16[32,2560]{1,0:T(8,128)(2,1)}, u32[]{:S(2)}) copy-start(bf16[32,2560]{1,0:T(8,128)(2,1)} %copy-done.25) | copy-start | bytes 491524
  (75 other events, 125.6 us)
Sparse Core Ops, SparseCore 0:
  117.6 21.0 reduce-scatter.8
  141.5 21.2 reduce-scatter.6
  258.5 22.1 reduce-scatter.12
  282.8 21.2 reduce-scatter.10
  306.8 65.4 reduce-scatter.16
  375.0 79.8 reduce-scatter.14
